TPU v7x, 32 devices: a whole 2x2x4 slice. The times are simulated.
32 devices in a mesh: row: 8 (over z, y), col: 4 (over x, core).
Axes of the slice: x: 2, y: 2, z: 4, core: 2. Of those that a mesh axis runs over, the one named last changes fastest.
Arguments:
- densities: bfloat16 [4608, 3072], P(('row', 'col')), may hold values from -0.796875 to 0.796875
- counts: int32 [512], P(('row', 'col')), may hold values from 3 to 9
- coulomb: float32 [3072], replicated, may hold values from 0.05 to 1
- energies: float32 [4608], P(('row', 'col')), may hold values from 8 to 64
- vectors: bfloat16 [4608, 64], P(('row', 'col')), may hold values from -0.09375 to 0.09375
Outputs:
- kernel: float32 [4608, 4608], P('row', 'col')
- product: float32 [4608, 64], P(('row', 'col'))
All inputs are finite; a program needn't handle non-finite values.
Results may differ from a plain program's by a relative error of at most 0.0095.
Values may be sent and summed in bfloat16 or wider, within the bound.
A program may use at most 128 MiB of HBM per device.

v0:
```python
import jax
import jax.numpy as jnp
from jax import lax
from jax.sharding import PartitionSpec as P

SLOT = 9


def body(densities, counts, coulomb, energies, vectors):
    kpoints = counts.shape[0]
    slot_index = lax.broadcasted_iota(jnp.int32, (kpoints, SLOT), 1)
    usable = (slot_index < counts[:, None]).reshape(kpoints * SLOT)
    masked = jnp.where(usable[:, None], densities, jnp.zeros_like(densities))
    weighted = (masked.astype(jnp.float32) * coulomb[None, :]).astype(jnp.bfloat16)
    row_block = lax.all_gather(weighted, "col", axis=0, tiled=True)
    kernel = lax.dot_general(
        row_block,
        lax.all_gather(masked, "row", axis=0, tiled=True),
        (((1,), (1,)), ((), ())),
        preferred_element_type=jnp.float32,
    )
    local_terms = lax.dot_general(
        masked, vectors, (((0,), (0,)), ((), ())), preferred_element_type=jnp.float32
    )
    projected = lax.psum(local_terms, ("row", "col"))
    coupled = jnp.dot(
        weighted.astype(jnp.float32),
        projected,
        precision=lax.Precision.HIGHEST,
        preferred_element_type=jnp.float32,
    )
    diagonal = jnp.where(usable, energies, jnp.zeros_like(energies))
    product = coupled + diagonal[:, None] * vectors.astype(jnp.float32)
    return (kernel, product)


def solution(mesh):
    return jax.shard_map(
        body,
        mesh=mesh,
        in_specs=(
            P(("row", "col"), None),
            P(("row", "col")),
            P(),
            P(("row", "col")),
            P(("row", "col"), None),
        ),
        out_specs=(P("row", "col"), P(("row", "col"), None)),
        check_vma=False,
    )
```

profile of v0, /device:TPU:0, one launch (start us, length us, event | category | flops | bytes accessed | tf_op | source)
XLA Modules:
  0.0 254.9 jit_solution(2723518301834246498)
XLA Ops:
  8.0 0.0 copy-start.2
  8.0 0.0 all-reduce.2.cloned.1.call-start
  8.1 0.7 iota_compare_fusion
  8.8 0.1 lt.18
  8.9 2.5 multiply_convert_fusion
  11.4 0.0 copy-start
  11.4 0.0 copy-done.2
  11.4 0.0 copy-start.3
  11.4 0.0 copy-start.1
  11.4 1.8 fusion.1
  13.2 0.0 all-reduce.2.cloned.1.call-update
  13.2 0.0 all-gather.3.cloned.1.call-start
  13.3 0.5 all-gather.3.cloned.1.call-update
  13.8 0.0 all-gather.5.cloned.1.call-start
  13.9 0.0 copy-done
  13.9 0.5 all-gather.5.cloned.1.call-update
  14.4 0.0 copy-done.3
  14.4 219.2 %all-reduce.2.cloned.1.call-done = f32[3072,64]{1,0:T(8,128)} async-done(((f32[3072,64]{1,0:T(8,128)}), f32[3072,64]{1,0:T(8,128)}) %all-reduce.2.cloned.1.call-update) | async-done | bytes 786448 | tf_op jit(solution)/shard_map/psum | solution.py:25
  233.7 0.0 copy-done.1
  233.7 3.5 %convolution_add_fusion = f32[144,64]{0,1:T(8,128)} fusion(bf16[144,3072]{1,0:T(8,128)(2,1)S(1)} %copy-done.1, f32[3072,64]{1,0:T(8,128)} %all-reduce.2.cloned.1.call-done, bf16[144,64]{0,1:T(8,128)(2,1)S(1)} %copy-done.2, f32[144]{0:T(256)S(1)} %broadcast_select_fusion.1), kind=kOutput, calls=%fused_computation.1 | convolution fusion | flops 339766272 | bytes 1727040 | tf_op jit(solution)/shard_map/dot_general | solution.py:26
  237.1 0.0 all-gather.3.cloned.1.call-done
  237.1 0.0 all-gather.5.cloned.1.call-done
  237.1 10.4 %fusion = f32[576,1152]{1,0:T(8,128)} fusion(bf16[576,3072]{1,0:T(8,128)(2,1)} %all-gather.3.cloned.1.call-done, bf16[1152,3072]{1,0:T(8,128)(2,1)} %all-gather.5.cloned.1.call-done), kind=kOutput, calls=%fused_computation.5 | convolution fusion | flops 4076863488 | bytes 13271040 | tf_op jit(solution)/shard_map/dot_general | solution.py:16
  (1 shorter events, 0.0 us)
Async XLA Ops:
  8.0 3.4 %copy-start.2 = (bf16[144,64]{0,1:T(8,128)(2,1)S(1)}, bf16[144,64]{0,1:T(8,128)(2,1)}, u32[]{:S(2)}) copy-start(bf16[144,64]{0,1:T(8,128)(2,1)} %param.9) | copy-start | bytes 55300
  8.0 225.6 %all-reduce.2.cloned.1.call-start = ((), (), s32[]{:S(2)}) async-start(), calls=%async_computation.2 | async-start | bytes 3145728 | tf_op jit(solution)/shard_map/psum | solution.py:25
  11.4 2.5 copy-start
  11.4 3.0 %copy-start.3 = (f32[144]{0:T(256)S(1)}, f32[144]{0:T(256)}, u32[]{:S(2)}) copy-start(f32[144]{0:T(256)} %param.8) | copy-start | bytes 1732
  11.4 222.2 %copy-start.1 = (bf16[144,3072]{1,0:T(8,128)(2,1)S(1)}, bf16[144,3072]{1,0:T(8,128)(2,1)}, u32[]{:S(2)}) copy-start(bf16[144,3072]{1,0:T(8,128)(2,1)} %get-tuple-element.2) | copy-start | bytes 2654212
  13.2 223.9 %all-gather.3.cloned.1.call-start = ((), (), s32[]{:S(2)}) async-start(), calls=%async_computation | async-start | bytes 4423680 | tf_op jit(solution)/shard_map/all_gather | solution.py:15
  13.8 223.3 %all-gather.5.cloned.1.call-start = ((), (), s32[]{:S(2)}) async-start(), calls=%async_computation.1 | async-start | bytes 7962624 | tf_op jit(solution)/shard_map/all_gather | solution.py:18
Sparse Core Ops, SparseCore 0:
  14.7 218.9 all-reduce.1
Sparse Core Ops, SparseCore 1:
  15.3 34.0 all-gather.2
  51.4 109.7 all-gather.4
where the time goes:
time: 255 us
  waiting for transfers between devices  220 us (86%)
  matrix products  15.6 us (6%)
  between operations  15.5 us (6%)
  other arithmetic  3.27 us (1%)
    psum x1, waiting for transfers between devices, body(): projected = lax.psum(local_terms, ('row', 'col'))  219 us
    dot_general x1, matrix products, body(): lax.dot_general(row_block, lax.all_gather(masked, 'row', axis=0, tiled=Tr...  10.4 us
  transfers between devices with their start and end apart: 3, of which 1 were waited for; matrix products, arithmetic and copies ran while one was open for 1% of the time, Pallas kernels for 0%

commit v1 on v0

v1 whole, which is shorter than its diff:
```python
import functools

import jax
import jax.numpy as jnp
from jax import lax
from jax.experimental import pallas as pl
from jax.experimental.pallas import tpu as pltpu
from jax.sharding import PartitionSpec as P

SLOT = 9
MESH = pl.DeviceIdType.MESH
NT = (((1,), (1,)), ((), ()))
TN = (((0,), (0,)), ((), ()))


def exchange_kernel(n_row, n_col, d_ref, v_ref, coulomb_ref, own_ref, part_ref, prod_ref,
                    cols, rows_raw, weighted, vecs, psend, q, qsend, qrecv, qpiece, qland,
                    local_sem, y_send, y_recv, up_send, down_send, z_recv, x_send, x_recv,
                    core_send, core_recv, v_send, v_recv, p_send, p_recv, q_send, q_recv, c_send, c_recv):
    line, chips = n_row // 2, n_col // 2
    r, c = lax.axis_index("row"), lax.axis_index("col")
    z, y = r // 2, lax.rem(r, 2)
    x, core = c // 2, lax.rem(c, 2)
    other_y, other_core = 1 - y, 1 - core
    block = d_ref.shape[1]
    nv = prod_ref.shape[0]

    barrier = pltpu.get_barrier_semaphore()
    for step in range(1, n_row):
        pl.semaphore_signal(barrier, inc=1, device_id=(lax.rem(r + step, n_row), c), device_id_type=MESH)
    for step in range(1, n_col):
        pl.semaphore_signal(barrier, inc=1, device_id=(r, lax.rem(c + step, n_col)), device_id_type=MESH)
    pl.semaphore_wait(barrier, n_row + n_col - 2)

    partner = (z * 2 + other_y, c)
    sibling = (r, x * 2 + other_core)

    def remote(src, dst, send, recv, device):
        return pltpu.make_async_remote_copy(
            src_ref=src, dst_ref=dst, send_sem=send, recv_sem=recv, device_id=device, device_id_type=MESH)

    def y_copy():
        return remote(d_ref.at[other_y], cols.at[z, y], y_send, y_recv, partner)

    def y_arrival():
        return remote(d_ref.at[other_y], cols.at[z, other_y], y_send, y_recv, partner)

    def up(src, zp, s):
        return remote(src, cols.at[zp, s], up_send.at[zp, s], z_recv.at[zp, s], ((z + 1) * 2 + y, c))

    def down(src, zp, s):
        return remote(src, cols.at[zp, s], down_send.at[zp, s], z_recv.at[zp, s], ((z - 1) * 2 + y, c))

    def x_copy(src, s, step):
        return remote(src, rows_raw.at[s, c], x_send.at[s, step], x_recv.at[s, x],
                      (r, lax.rem(x + step, chips) * 2 + core))

    def x_arrival(s, step):
        xs = lax.rem(x + chips - step, chips)
        return remote(d_ref.at[0], rows_raw.at[s, xs * 2 + core], x_send.at[s, step], x_recv.at[s, xs], sibling)

    def core_copy(src, s, xs):
        return remote(src, rows_raw.at[s, xs * 2 + core], core_send.at[s, xs], core_recv.at[s, xs], sibling)

    def core_arrival(s, xs):
        return remote(d_ref.at[0], rows_raw.at[s, xs * 2 + other_core], core_send.at[s, xs], core_recv.at[s, xs],
                      sibling)

    def spread(src, s):
        @pl.when(z < line - 1)
        def _():
            up(src, z, s).start()

        @pl.when(z > 0)
        def _():
            down(src, z, s).start()

        for step in range(1, chips):
            x_copy(src, s, step).start()
        core_copy(src, s, x).start()

    def relay(zp, s):
        @pl.when((zp < z) & (z < line - 1))
        def _():
            up(cols.at[zp, s], zp, s).start()

        @pl.when((zp > z) & (z > 0))
        def _():
            down(cols.at[zp, s], zp, s).start()

    def z_wait(zp, s):
        remote(cols.at[zp, s], cols.at[zp, s], up_send.at[zp, s], z_recv.at[zp, s], sibling).wait_recv()

    y_copy().start()
    spread(d_ref.at[y], y)
    for step in range(1, n_row):
        remote(v_ref, vecs.at[r], v_send.at[step], v_recv.at[r], (lax.rem(r + step, n_row), c)).start()
    locals_ = [
        pltpu.make_async_copy(d_ref.at[y], cols.at[z, y], local_sem.at[0]),
        pltpu.make_async_copy(d_ref.at[y], rows_raw.at[y, c], local_sem.at[1]),
        pltpu.make_async_copy(v_ref, vecs.at[r], local_sem.at[2]),
    ]
    for copy in locals_:
        copy.start()
    q[...] = jnp.zeros_like(q)
    for copy in locals_:
        copy.wait()

    y_arrival().wait_recv()
    spread(cols.at[z, other_y], other_y)
    late = pltpu.make_async_copy(cols.at[z, other_y], rows_raw.at[other_y, c], local_sem.at[3])
    late.start()

    def share(s):
        for step in range(1, chips):
            xs = lax.rem(x + chips - step, chips)
            x_arrival(s, step).wait_recv()
            core_copy(rows_raw.at[s, xs * 2 + core], s, xs).start()

    def weigh(s):
        for xs in range(chips):
            core_arrival(s, xs).wait_recv()
        for cp in range(n_col):
            weighted[s, cp * block:(cp + 1) * block, :] = (
                rows_raw[s, cp].astype(jnp.float32) * coulomb_ref[y]).astype(jnp.bfloat16)

    share(y)
    for zp in (z - 1, z + 1):
        @pl.when((zp >= 0) & (zp < line))
        def _():
            z_wait(zp, y)
            relay(zp, y)
    weigh(y)
    late.wait()
    share(other_y)
    weigh(other_y)
    for step in range(1, n_row):
        rp = lax.rem(r + step, n_row)
        remote(v_ref, vecs.at[rp], v_send.at[step], v_recv.at[rp], partner).wait_recv()

    def p_copy(rp):
        return remote(psend.at[rp], part_ref.at[rp], p_send.at[rp], p_recv.at[rp], partner)

    def tile(t, carry):
        first = t < 2
        u = jnp.where(first, 0, t - 2)
        d = jnp.where(first, 0, u // 4 + 1)
        turn = jnp.where(first, t, lax.rem(u // 2, 2))
        side = 2 * lax.rem(u, 2) - 1
        zp = z + d * side
        s = jnp.where(turn == 0, y, other_y)

        @pl.when((zp >= 0) & (zp < line))
        def _():
            @pl.when((d > 1) | ((d == 1) & (turn == 1)))
            def _():
                z_wait(zp, s)
                relay(zp, s)

            rp = zp * 2 + s
            away = lax.dot_general(cols[zp, s], weighted[other_y], NT,
                                   preferred_element_type=jnp.float32).astype(jnp.bfloat16)
            psend[rp] = away
            packed = vecs[rp].astype(jnp.float32)
            v = jnp.concatenate([packed[:, :nv], packed[:, nv:]], axis=0).astype(jnp.bfloat16)
            home = lax.dot_general(cols[zp, s], weighted[y], NT, preferred_element_type=jnp.float32)
            own_ref[rp] = home
            p_copy(rp).start()
            q[1] += lax.dot_general(v, away, TN, preferred_element_type=jnp.float32)
            q[0] += lax.dot_general(v, home.astype(jnp.bfloat16), TN, preferred_element_type=jnp.float32)
        return carry

    lax.fori_loop(0, 2 + 4 * (line - 1), tile, 0)

    qsend[...] = q[1].astype(jnp.bfloat16)
    q_copy = remote(qsend, qrecv, q_send, q_recv, partner)
    q_copy.start()
    q_copy.wait()
    total = q[0] + qrecv[...].astype(jnp.float32)
    for cp in range(n_col):
        qpiece[cp] = total[:, cp * block:(cp + 1) * block].astype(jnp.bfloat16)

    def c_copy(step):
        to = lax.rem(c + step, n_col)
        return remote(qpiece.at[to], qland.at[c], c_send.at[step], c_recv.at[c], (r, to))

    for step in range(1, n_col):
        c_copy(step).start()
    answer = qpiece[c].astype(jnp.float32)
    for step in range(1, n_col):
        source = lax.rem(c + step, n_col)
        remote(qpiece.at[0], qland.at[source], c_send.at[step], c_recv.at[source], sibling).wait_recv()
        answer += qland[source].astype(jnp.float32)
    prod_ref[...] = answer

    y_copy().wait_send()
    for step in range(1, n_col):
        c_copy(step).wait_send()
    for step in range(1, n_row):
        remote(v_ref, vecs.at[r], v_send.at[step], v_recv.at[r], partner).wait_send()
    for s in range(2):
        for step in range(1, chips):
            x_copy(d_ref.at[0], s, step).wait_send()
        for xs in range(chips):
            core_copy(d_ref.at[0], s, xs).wait_send()
        for zp in range(line):
            @pl.when((zp <= z) & (z < line - 1))
            def _():
                up(d_ref.at[0], zp, s).wait_send()

            @pl.when((zp >= z) & (z > 0))
            def _():
                down(d_ref.at[0], zp, s).wait_send()
    for rp in range(n_row):
        p_copy(rp).wait()


def body(n_row, n_col, densities, counts, coulomb, energies, vectors):
    rows, depth = densities.shape
    nv = vectors.shape[1]
    half = depth // 2
    line, chips = n_row // 2, n_col // 2
    slot_index = lax.broadcasted_iota(jnp.int32, (counts.shape[0], SLOT), 1)
    usable = (slot_index < counts[:, None]).reshape(rows)
    masked = jnp.where(usable[:, None], densities, jnp.zeros_like(densities))
    halves = jnp.stack([masked[:, :half], masked[:, half:]])
    packed = jnp.concatenate([vectors[:rows // 2], vectors[rows // 2:]], axis=1)
    bf16, f32 = jnp.bfloat16, jnp.float32
    vmem = pl.BlockSpec(memory_space=pltpu.VMEM)
    dma = pltpu.SemaphoreType.DMA
    wide = n_col * rows
    own, part, prod = pl.pallas_call(
        functools.partial(exchange_kernel, n_row, n_col),
        out_shape=(
            jax.ShapeDtypeStruct((n_row, rows, wide), f32),
            jax.ShapeDtypeStruct((n_row, rows, wide), bf16),
            jax.ShapeDtypeStruct((nv, rows), f32),
        ),
        in_specs=[vmem] * 3,
        out_specs=(vmem, vmem, vmem),
        scratch_shapes=[
            pltpu.VMEM((line, 2, rows, half), bf16),
            pltpu.VMEM((2, n_col, rows, half), bf16),
            pltpu.VMEM((2, wide, half), bf16),
            pltpu.VMEM((n_row,) + packed.shape, bf16),
            pltpu.VMEM((n_row, rows, wide), bf16),
            pltpu.VMEM((2, nv, wide), f32),
            pltpu.VMEM((nv, wide), bf16),
            pltpu.VMEM((nv, wide), bf16),
            pltpu.VMEM((n_col, nv, rows), bf16),
            pltpu.VMEM((n_col, nv, rows), bf16),
            dma((4,)), dma, dma, dma((line, 2)), dma((line, 2)), dma((line, 2)),
            dma((2, chips)), dma((2, chips)), dma((2, chips)), dma((2, chips)),
            dma((n_row,)), dma((n_row,)), dma((n_row,)), dma((n_row,)), dma, dma,
            dma((n_col,)), dma((n_col,)),
        ],
        compiler_params=pltpu.CompilerParams(
            collective_id=0, has_side_effects=True, vmem_limit_bytes=60 * 2**20),
    )(halves, packed, coulomb.reshape(2, 1, half))
    kernel = (own + part.astype(f32)).reshape(n_row * rows, wide).T
    diagonal = jnp.where(usable, energies, jnp.zeros_like(energies))
    product = prod.T + diagonal[:, None] * vectors.astype(f32)
    return (kernel, product)


def solution(mesh):
    return jax.shard_map(
        functools.partial(body, mesh.shape["row"], mesh.shape["col"]),
        mesh=mesh,
        in_specs=(
            P(("row", "col"), None),
            P(("row", "col")),
            P(),
            P(("row", "col")),
            P(("row", "col"), None),
        ),
        out_specs=(P("row", "col"), P(("row", "col"), None)),
        check_vma=False,
    )
```

time: 255 us -> 92.7 us (0.36)
  waiting for transfers between devices: 220 us -> 0 us
  Pallas kernels: 0 us -> 82.1 us
  matrix products: 15.6 us -> 0 us
  between operations: 15.5 us -> 0.71 us
  other arithmetic: 3.27 us -> 6.87 us
  local copies, waits for them, and re-layouts: 0.11 us -> 2.74 us
    psum x1 -> x0, waiting for transfers between devices: 219 us -> none  [body(): projected = lax.psum(local_terms, ('row', 'col'))]
    pallas_call x0 -> x1, Pallas kernels: none -> 82.1 us  [body(): pl.pallas_call(functools.partial(exchange_kernel, n_row, n_col), out_shap...]
    dot_general x3 -> x0, matrix products: 15.6 us -> none  [the longest x1 10.4 us: body(): lax.dot_general(row_block, lax.all_gather(masked, 'row', axis=0, tiled=Tr...]
    add x0 -> x2, other arithmetic: none -> 3.15 us  [the longest x1 2.51 us: body(): kernel = (own + part.astype(f32)).reshape(n_row * rows, wide).T]
  transfers between devices with their start and end apart: 3 -> 0, of which waited for: 1 -> 0; matrix products, arithmetic and copies ran while one was open for 1% -> 0% of each run, Pallas kernels for 0% -> 0%
where the time goes in v1:
time: 92.7 us; the launch traced here: 92.4 us
  Pallas kernels  82.1 us (89%)
  other arithmetic  6.87 us (7%)
  local copies, waits for them, and re-layouts  2.74 us (3%)
    pallas_call x1, Pallas kernels, body(): pl.pallas_call(functools.partial(exchange_kernel, n_row, n_col), out_shap...  82.1 us
    add x1, other arithmetic, body(): kernel = (own + part.astype(f32)).reshape(n_row * rows, wide).T  2.51 us
    reshape x1, local copies, waits for them, and re-layouts, body(): kernel = (own + part.astype(f32)).reshape(n_row * rows, wide).T  2.3 us

profile of v1, /device:TPU:0, one launch (start us, length us, event | category | flops | bytes accessed | tf_op | source)
XLA Modules:
  0.0 92.4 jit_solution(13125262689874957929)
XLA Ops:
  0.6 0.0 copy-start
  0.6 0.7 iota_compare_fusion
  1.4 0.1 lt.18
  1.5 1.3 %broadcast_select_fusion = bf16[144,3072]{1,0:T(8,128)(2,1)S(1)} fusion(bf16[144,3072]{1,0:T(8,128)(2,1)} %param.5, pred[144]{0:T(512)(128)(4,1)S(1)} %lt.18), kind=kLoop, calls=%fused_computation.2 | loop fusion | flops 442368 | bytes 1769616 | tf_op jit(solution)/shard_map/jit(_where)/select_n | solution.py:225
  2.8 0.1 slice_bitcast_fusion.1
  2.8 1.0 %pad_maximum_fusion.d_ref = bf16[2,144,1536]{2,1,0:T(8,128)(2,1)} fusion(bf16[1,144,1536]{2,1,0:T(8,128)(2,1)S(1)} %get-tuple-element.9, bf16[1,144,1536]{2,1,0:T(8,128)(2,1)S(1)} %get-tuple-element.8), kind=kLoop, calls=%fused_computation.1 | loop fusion | flops 442368 | bytes 1769472 | tf_op jit(solution)/shard_map/stack | solution.py:226
  3.8 0.0 copy-done
  3.8 0.1 fusion
  3.9 0.1 copy.10
  4.0 0.1 copy.11
  4.1 0.7 pad_maximum_fusion.1.v_ref
  4.8 82.1 %shard_map.68 = (f32[8,144,576]{2,1,0:T(8,128)}, bf16[8,144,576]{2,1,0:T(8,128)(2,1)}, f32[64,144]{1,0:T(8,128)}) custom-call(bf16[2,144,1536]{2,1,0:T(8,128)(2,1)} %pad_maximum_fusion.d_ref, bf16[72,128]{1,0:T(8,128)(2,1)} %pad_maximum_fusion.1.v_ref, f32[2,1,1536]{2,1,0:T(1,128)} %bitcast.11), custom_call_target="tpu_custom_call" | custom-call | tf_op jit(solution)/shard_map/pallas_call | solution.py:232
  86.9 2.5 %convert_add_fusion = f32[8,144,576]{2,1,0:T(8,128)S(1)} fusion(f32[8,144,576]{2,1,0:T(8,128)} %get-tuple-element.5, bf16[8,144,576]{2,1,0:T(8,128)(2,1)} %get-tuple-element.6), kind=kLoop, calls=%fused_computation | loop fusion | flops 1327104 | bytes 6635520 | tf_op jit(solution)/shard_map/add | solution.py:260
  89.4 0.0 copy-start.2
  89.4 0.0 copy-start.1
  89.5 2.3 %copy.9 = f32[1152,576]{0,1:T(8,128)} copy(f32[1152,576]{1,0:T(8,128)S(1)} %bitcast.9) | data formatting | bytes 5308416 | tf_op jit(solution)/shard_map/reshape | solution.py:260
  91.8 0.0 copy-done.2
  91.8 0.0 copy-done.1
  91.8 0.6 bitcast_add_fusion
  (1 shorter events, 0.0 us)
Async XLA Ops:
  0.6 3.2 %copy-start = (bf16[144,64]{0,1:T(8,128)(2,1)S(1)}, bf16[144,64]{0,1:T(8,128)(2,1)}, u32[]{:S(2)}) copy-start(bf16[144,64]{0,1:T(8,128)(2,1)} %param.9) | copy-start | bytes 55300
  89.4 2.3 %copy-start.2 = (f32[144]{0:T(256)S(1)}, f32[144]{0:T(256)}, u32[]{:S(2)}) copy-start(f32[144]{0:T(256)} %param.8) | copy-start | bytes 1732
  89.4 2.3 %copy-start.1 = (f32[64,144]{1,0:T(8,128)S(1)}, f32[64,144]{1,0:T(8,128)}, u32[]{:S(2)}) copy-start(f32[64,144]{1,0:T(8,128)} %get-tuple-element.7) | copy-start | bytes 110596

commit v2 on v1

--- a/solution.py
+++ b/solution.py
@@ -10,11 +10,27 @@
 SLOT = 9
 MESH = pl.DeviceIdType.MESH
 NT = (((1,), (1,)), ((), ()))
-TN = (((0,), (0,)), ((), ()))
-
-
-def exchange_kernel(n_row, n_col, d_ref, v_ref, coulomb_ref, own_ref, part_ref, prod_ref,
-                    cols, rows_raw, weighted, vecs, psend, q, qsend, qrecv, qpiece, qland,
+NN = (((1,), (0,)), ((), ()))
+
+
+def pack(v):
+    lanes = 128
+    rest = v.shape[1] % lanes
+    height = v.shape[0] * rest // lanes
+    tail = jnp.concatenate(
+        [v[j * height:(j + 1) * height, lanes:] for j in range(lanes // rest)], axis=1)
+    return jnp.concatenate([v[:, :lanes], tail], axis=0)
+
+
+def unpack(p, nv, rest):
+    lanes = 128
+    tail = jnp.concatenate(
+        [p[nv:, j * rest:(j + 1) * rest] for j in range(lanes // rest)], axis=0)
+    return jnp.concatenate([p[:nv], tail], axis=1)
+
+
+def exchange_kernel(n_row, n_col, raw_ref, counts_ref, energies_ref, vt_ref, coulomb_ref, own_ref, part_ref, prod_ref,
+                    d_ref, v_ref, cols, rows_raw, weighted, vecs, psend, q, qsend, qrecv, qpiece, qland,
                     local_sem, y_send, y_recv, up_send, down_send, z_recv, x_send, x_recv,
                     core_send, core_recv, v_send, v_recv, p_send, p_recv, q_send, q_recv, c_send, c_recv):
     line, chips = n_row // 2, n_col // 2
@@ -23,6 +39,7 @@
     x, core = c // 2, lax.rem(c, 2)
     other_y, other_core = 1 - y, 1 - core
     block = d_ref.shape[1]
+    half = d_ref.shape[2]
     nv = prod_ref.shape[0]
 
     barrier = pltpu.get_barrier_semaphore()
@@ -30,6 +47,19 @@
         pl.semaphore_signal(barrier, inc=1, device_id=(lax.rem(r + step, n_row), c), device_id_type=MESH)
     for step in range(1, n_col):
         pl.semaphore_signal(barrier, inc=1, device_id=(r, lax.rem(c + step, n_col)), device_id_type=MESH)
+
+    kpoints = counts_ref.shape[1]
+    counts = counts_ref[...].astype(jnp.float32)
+    row_index = lax.broadcasted_iota(jnp.int32, (block, kpoints), 0)
+    kpoint = lax.broadcasted_iota(jnp.int32, (block, kpoints), 1)
+    slot = row_index - SLOT * kpoint
+    inside = (slot >= 0) & (slot < SLOT) & (slot.astype(jnp.float32) < counts)
+    usable = jnp.sum(jnp.where(inside, 1.0, 0.0), axis=1, keepdims=True)
+    for part in range(2):
+        piece = raw_ref[:, part * half:(part + 1) * half].astype(jnp.float32)
+        d_ref[part] = jnp.where(usable > 0.5, piece, 0.0).astype(jnp.bfloat16)
+    vt = vt_ref[...].astype(jnp.float32)
+    v_ref[...] = pack(vt).astype(jnp.bfloat16)
     pl.semaphore_wait(barrier, n_row + n_col - 2)
 
     partner = (z * 2 + other_y, c)
@@ -161,13 +191,12 @@
             away = lax.dot_general(cols[zp, s], weighted[other_y], NT,
                                    preferred_element_type=jnp.float32).astype(jnp.bfloat16)
             psend[rp] = away
-            packed = vecs[rp].astype(jnp.float32)
-            v = jnp.concatenate([packed[:, :nv], packed[:, nv:]], axis=0).astype(jnp.bfloat16)
+            v = unpack(vecs[rp].astype(jnp.float32), nv, block % 128).astype(jnp.bfloat16)
             home = lax.dot_general(cols[zp, s], weighted[y], NT, preferred_element_type=jnp.float32)
             own_ref[rp] = home
             p_copy(rp).start()
-            q[1] += lax.dot_general(v, away, TN, preferred_element_type=jnp.float32)
-            q[0] += lax.dot_general(v, home.astype(jnp.bfloat16), TN, preferred_element_type=jnp.float32)
+            q[1] += lax.dot_general(v, away, NN, preferred_element_type=jnp.float32)
+            q[0] += lax.dot_general(v, home.astype(jnp.bfloat16), NN, preferred_element_type=jnp.float32)
         return carry
 
     lax.fori_loop(0, 2 + 4 * (line - 1), tile, 0)
@@ -191,7 +220,13 @@
         source = lax.rem(c + step, n_col)
         remote(qpiece.at[0], qland.at[source], c_send.at[step], c_recv.at[source], sibling).wait_recv()
         answer += qland[source].astype(jnp.float32)
-    prod_ref[...] = answer
+    lane_slot = (lax.broadcasted_iota(jnp.int32, (kpoints, block), 1)
+                 - SLOT * lax.broadcasted_iota(jnp.int32, (kpoints, block), 0))
+    mine = jnp.where((lane_slot >= 0) & (lane_slot < SLOT), 1.0, 0.0)
+    limit = lax.dot_general(jnp.broadcast_to(counts, (8, kpoints)), mine, NN, preferred_element_type=jnp.float32)[:1]
+    lane_slot = lax.rem(lax.broadcasted_iota(jnp.int32, (1, block), 1), SLOT).astype(jnp.float32)
+    diagonal = jnp.where(lane_slot + 0.5 < limit, energies_ref[...], 0.0)
+    prod_ref[...] = answer + diagonal * vt_ref[...].astype(jnp.float32)
 
     y_copy().wait_send()
     for step in range(1, n_col):
@@ -215,17 +250,19 @@
         p_copy(rp).wait()
 
 
+def assemble_kernel(own_ref, part_ref, out_ref):
+    n_row, rows, chunk = own_ref.shape
+    total = own_ref[...] + part_ref[...].astype(jnp.float32)
+    out_ref[...] = total.reshape(n_row * rows, chunk).T
+
+
 def body(n_row, n_col, densities, counts, coulomb, energies, vectors):
     rows, depth = densities.shape
     nv = vectors.shape[1]
     half = depth // 2
     line, chips = n_row // 2, n_col // 2
-    slot_index = lax.broadcasted_iota(jnp.int32, (counts.shape[0], SLOT), 1)
-    usable = (slot_index < counts[:, None]).reshape(rows)
-    masked = jnp.where(usable[:, None], densities, jnp.zeros_like(densities))
-    halves = jnp.stack([masked[:, :half], masked[:, half:]])
-    packed = jnp.concatenate([vectors[:rows // 2], vectors[rows // 2:]], axis=1)
     bf16, f32 = jnp.bfloat16, jnp.float32
+    packed = jax.eval_shape(pack, jax.ShapeDtypeStruct((nv, rows), bf16))
     vmem = pl.BlockSpec(memory_space=pltpu.VMEM)
     dma = pltpu.SemaphoreType.DMA
     wide = n_col * rows
@@ -236,9 +273,11 @@
             jax.ShapeDtypeStruct((n_row, rows, wide), bf16),
             jax.ShapeDtypeStruct((nv, rows), f32),
         ),
-        in_specs=[vmem] * 3,
+        in_specs=[vmem] * 5,
         out_specs=(vmem, vmem, vmem),
         scratch_shapes=[
+            pltpu.VMEM((2, rows, half), bf16),
+            pltpu.VMEM(packed.shape, bf16),
             pltpu.VMEM((line, 2, rows, half), bf16),
             pltpu.VMEM((2, n_col, rows, half), bf16),
             pltpu.VMEM((2, wide, half), bf16),
@@ -256,11 +295,16 @@
         ],
         compiler_params=pltpu.CompilerParams(
             collective_id=0, has_side_effects=True, vmem_limit_bytes=60 * 2**20),
-    )(halves, packed, coulomb.reshape(2, 1, half))
-    kernel = (own + part.astype(f32)).reshape(n_row * rows, wide).T
-    diagonal = jnp.where(usable, energies, jnp.zeros_like(energies))
-    product = prod.T + diagonal[:, None] * vectors.astype(f32)
-    return (kernel, product)
+    )(densities, counts[None], energies[None], vectors.T, coulomb.reshape(2, 1, half))
+    chunk = 128
+    kernel = pl.pallas_call(
+        assemble_kernel,
+        out_shape=jax.ShapeDtypeStruct((wide, n_row * rows), f32),
+        grid=(pl.cdiv(wide, chunk),),
+        in_specs=[pl.BlockSpec((n_row, rows, chunk), lambda i: (0, 0, i))] * 2,
+        out_specs=pl.BlockSpec((chunk, n_row * rows), lambda i: (i, 0)),
+    )(own, part)
+    return (kernel, prod.T)
 
 
 def solution(mesh):

time: 92.7 us -> 89.5 us (0.965)
  other arithmetic: 6.87 us -> 0 us
  Pallas kernels: 82.1 us -> 88 us
  local copies, waits for them, and re-layouts: 2.74 us -> 0.63 us
    pallas_call x0 -> x1, Pallas kernels: none -> 5.74 us  [body(): pl.pallas_call(assemble_kernel, out_shape=jax.ShapeDtypeStruct((wide, n_r...]
    add x2 -> x0, other arithmetic: 3.15 us -> none  [the longest x1 2.51 us: body(): kernel = (own + part.astype(f32)).reshape(n_row * rows, wide).T]
    reshape x1 -> x0, local copies, waits for them, and re-layouts: 2.3 us -> none  [body(): kernel = (own + part.astype(f32)).reshape(n_row * rows, wide).T]
    select_n x2 -> x0, other arithmetic: 1.3 us -> none  [the longest x1 1.3 us: body(): masked = jnp.where(usable[:, None], densities, jnp.zeros_like(densities))]
    another operation x1 -> x0, other arithmetic: 0.99 us -> none  [body(): halves = jnp.stack([masked[:, :half], masked[:, half:]])]
where the time goes in v2:
time: 89.5 us; the launch traced here: 89.2 us
  Pallas kernels  88 us (98%)
    pallas_call x1, Pallas kernels, body(): pl.pallas_call(functools.partial(exchange_kernel, n_row, n_col), out_shap...  82.2 us
    pallas_call x1, Pallas kernels, body(): pl.pallas_call(assemble_kernel, out_shape=jax.ShapeDtypeStruct((wide, n_r...  5.74 us

profile of v2, /device:TPU:0, one launch (start us, length us, event | category | flops | bytes accessed | tf_op | source)
XLA Modules:
  0.0 89.2 jit_solution(11565393831553708782)
XLA Ops:
  0.6 82.2 %shard_map.68 = (f32[8,144,576]{2,1,0:T(8,128)}, bf16[8,144,576]{2,1,0:T(8,128)(2,1)}, f32[64,144]{1,0:T(8,128)}) custom-call(bf16[144,3072]{1,0:T(8,128)(2,1)} %raw_ref.1, s32[1,16]{1,0:T(1,128)} %bitcast.9, f32[1,144]{1,0:T(1,128)} %bitcast.8, bf16[64,144]{1,0:T(8,128)(2,1)} %bitcast.6, f32[2,1,1536]{2,1,0:T(1,128)} %bitcast.7), custom_call_target="tpu_custom_call" | custom-call | tf_op jit(solution)/shard_map/pallas_call | solution.py:269
  82.9 0.0 copy-start
  82.9 5.7 %shard_map.69 = f32[576,1152]{1,0:T(8,128)} custom-call(f32[8,144,576]{2,1,0:T(8,128)} %get-tuple-element.5.own_ref, bf16[8,144,576]{2,1,0:T(8,128)(2,1)} %get-tuple-element.6.part_ref), custom_call_target="tpu_custom_call" | custom-call | tf_op jit(solution)/shard_map/pallas_call | solution.py:300
  88.6 0.0 copy-done
  88.6 0.6 copy.8
Async XLA Ops:
  82.9 5.8 %copy-start = (f32[64,144]{1,0:T(8,128)S(1)}, f32[64,144]{1,0:T(8,128)}, u32[]{:S(2)}) copy-start(f32[64,144]{1,0:T(8,128)} %get-tuple-element.7) | copy-start | bytes 110596

commit v3 on v2

--- a/solution.py
+++ b/solution.py
@@ -154,15 +154,19 @@
             weighted[s, cp * block:(cp + 1) * block, :] = (
                 rows_raw[s, cp].astype(jnp.float32) * coulomb_ref[y]).astype(jnp.bfloat16)
 
+    def neighbours(s):
+        for zp in (z - 1, z + 1):
+            @pl.when((zp >= 0) & (zp < line))
+            def _():
+                z_wait(zp, s)
+                relay(zp, s)
+
     share(y)
-    for zp in (z - 1, z + 1):
-        @pl.when((zp >= 0) & (zp < line))
-        def _():
-            z_wait(zp, y)
-            relay(zp, y)
+    neighbours(y)
     weigh(y)
     late.wait()
     share(other_y)
+    neighbours(other_y)
     weigh(other_y)
     for step in range(1, n_row):
         rp = lax.rem(r + step, n_row)
@@ -171,39 +175,66 @@
     def p_copy(rp):
         return remote(psend.at[rp], part_ref.at[rp], p_send.at[rp], p_recv.at[rp], partner)
 
-    def tile(t, carry):
-        first = t < 2
-        u = jnp.where(first, 0, t - 2)
-        d = jnp.where(first, 0, u // 4 + 1)
-        turn = jnp.where(first, t, lax.rem(u // 2, 2))
-        side = 2 * lax.rem(u, 2) - 1
-        zp = z + d * side
-        s = jnp.where(turn == 0, y, other_y)
+    def vector(rp):
+        return unpack(vecs[rp].astype(jnp.float32), nv, block % 128).astype(jnp.bfloat16)
+
+    def pair(t, carry):
+        zp = z + jnp.where(t == 0, 0, 2 * t - 3)
 
         @pl.when((zp >= 0) & (zp < line))
         def _():
-            @pl.when((d > 1) | ((d == 1) & (turn == 1)))
-            def _():
-                z_wait(zp, s)
-                relay(zp, s)
-
+            both = cols[zp].reshape(2 * block, half)
+            away = lax.dot_general(both, weighted[other_y], NT,
+                                   preferred_element_type=jnp.float32).astype(jnp.bfloat16)
+            for s in range(2):
+                tile = away[s * block:(s + 1) * block]
+                psend[zp * 2 + s] = tile
+                q[1] += lax.dot_general(vector(zp * 2 + s), tile, NN, preferred_element_type=jnp.float32)
+            for s in range(2):
+                p_copy(zp * 2 + s).start()
+            home = lax.dot_general(both, weighted[y], NT, preferred_element_type=jnp.float32)
+            for s in range(2):
+                tile = home[s * block:(s + 1) * block]
+                own_ref[zp * 2 + s] = tile
+                q[0] += lax.dot_general(vector(zp * 2 + s), tile.astype(jnp.bfloat16), NN,
+                                        preferred_element_type=jnp.float32)
+        return carry
+
+    lax.fori_loop(0, 3, pair, 0)
+
+    q_copy = remote(qsend, qrecv, q_send, q_recv, partner)
+    slots = 4 * (line - 2)
+    last = jnp.where(z == 0, slots - 1, jnp.where(z == line - 1, slots - 2, 4 * (jnp.maximum(z, line - 1 - z) - 2) + 2
+                     + jnp.where(z < line - 1 - z, 1, 0)))
+
+    def single(t, carry):
+        d = t // 4 + 2
+        s = jnp.where(lax.rem(t // 2, 2) == 0, y, other_y)
+        zp = z + d * (2 * lax.rem(t, 2) - 1)
+
+        @pl.when((zp >= 0) & (zp < line))
+        def _():
+            z_wait(zp, s)
+            relay(zp, s)
             rp = zp * 2 + s
+            v = vector(rp)
             away = lax.dot_general(cols[zp, s], weighted[other_y], NT,
                                    preferred_element_type=jnp.float32).astype(jnp.bfloat16)
             psend[rp] = away
-            v = unpack(vecs[rp].astype(jnp.float32), nv, block % 128).astype(jnp.bfloat16)
+            q[1] += lax.dot_general(v, away, NN, preferred_element_type=jnp.float32)
+
+            @pl.when(t == last)
+            def _():
+                qsend[...] = q[1].astype(jnp.bfloat16)
+                q_copy.start()
+
+            p_copy(rp).start()
             home = lax.dot_general(cols[zp, s], weighted[y], NT, preferred_element_type=jnp.float32)
             own_ref[rp] = home
-            p_copy(rp).start()
-            q[1] += lax.dot_general(v, away, NN, preferred_element_type=jnp.float32)
             q[0] += lax.dot_general(v, home.astype(jnp.bfloat16), NN, preferred_element_type=jnp.float32)
         return carry
 
-    lax.fori_loop(0, 2 + 4 * (line - 1), tile, 0)
-
-    qsend[...] = q[1].astype(jnp.bfloat16)
-    q_copy = remote(qsend, qrecv, q_send, q_recv, partner)
-    q_copy.start()
+    lax.fori_loop(0, slots, single, 0)
     q_copy.wait()
     total = q[0] + qrecv[...].astype(jnp.float32)
     for cp in range(n_col):

time: 89.5 us -> 86.1 us (0.962)
  Pallas kernels: 88 us -> 84.6 us
    pallas_call x1, Pallas kernels: 82.2 us -> 78.9 us  [body(): pl.pallas_call(functools.partial(exchange_kernel, n_row, n_col), out_shap...]
where the time goes in v3:
time: 86.1 us; the launch traced here: 85.9 us
  Pallas kernels  84.6 us (98%)
    pallas_call x1, Pallas kernels, body(): pl.pallas_call(functools.partial(exchange_kernel, n_row, n_col), out_shap...  78.9 us
    pallas_call x1, Pallas kernels, body(): pl.pallas_call(assemble_kernel, out_shape=jax.ShapeDtypeStruct((wide, n_r...  5.74 us

profile of v3, /device:TPU:0, one launch (start us, length us, event | category | flops | bytes accessed | tf_op | source)
XLA Modules:
  0.0 85.9 jit_solution(6950760445832192155)
XLA Ops:
  0.6 78.9 %shard_map.68 = (f32[8,144,576]{2,1,0:T(8,128)}, bf16[8,144,576]{2,1,0:T(8,128)(2,1)}, f32[64,144]{1,0:T(8,128)}) custom-call(bf16[144,3072]{1,0:T(8,128)(2,1)} %raw_ref.1, s32[1,16]{1,0:T(1,128)} %bitcast.9, f32[1,144]{1,0:T(1,128)} %bitcast.8, bf16[64,144]{1,0:T(8,128)(2,1)} %bitcast.6, f32[2,1,1536]{2,1,0:T(1,128)} %bitcast.7), custom_call_target="tpu_custom_call" | custom-call | tf_op jit(solution)/shard_map/pallas_call | solution.py:300
  79.5 0.0 copy-start
  79.5 5.7 %shard_map.69 = f32[576,1152]{1,0:T(8,128)} custom-call(f32[8,144,576]{2,1,0:T(8,128)} %get-tuple-element.5.own_ref, bf16[8,144,576]{2,1,0:T(8,128)(2,1)} %get-tuple-element.6.part_ref), custom_call_target="tpu_custom_call" | custom-call | tf_op jit(solution)/shard_map/pallas_call | solution.py:331
  85.2 0.0 copy-done
  85.2 0.6 copy.8
Async XLA Ops:
  79.5 5.8 %copy-start = (f32[64,144]{1,0:T(8,128)S(1)}, f32[64,144]{1,0:T(8,128)}, u32[]{:S(2)}) copy-start(f32[64,144]{1,0:T(8,128)} %get-tuple-element.7) | copy-start | bytes 110596

commit v4 on v3

--- a/solution.py
+++ b/solution.py
@@ -29,8 +29,8 @@
     return jnp.concatenate([p[:nv], tail], axis=1)
 
 
-def exchange_kernel(n_row, n_col, raw_ref, counts_ref, energies_ref, vt_ref, coulomb_ref, own_ref, part_ref, prod_ref,
-                    d_ref, v_ref, cols, rows_raw, weighted, vecs, psend, q, qsend, qrecv, qpiece, qland,
+def exchange_kernel(n_row, n_col, raw_ref, counts_ref, energies_ref, vt_ref, coulomb_ref, out_ref, prod_ref,
+                    own_ref, part_ref, d_ref, v_ref, cols, rows_raw, weighted, vecs, psend, q, qsend, qrecv, qpiece, qland,
                     local_sem, y_send, y_recv, up_send, down_send, z_recv, x_send, x_recv,
                     core_send, core_recv, v_send, v_recv, p_send, p_recv, q_send, q_recv, c_send, c_recv):
     line, chips = n_row // 2, n_col // 2
@@ -204,8 +204,29 @@
 
     q_copy = remote(qsend, qrecv, q_send, q_recv, partner)
     slots = 4 * (line - 2)
-    last = jnp.where(z == 0, slots - 1, jnp.where(z == line - 1, slots - 2, 4 * (jnp.maximum(z, line - 1 - z) - 2) + 2
-                     + jnp.where(z < line - 1 - z, 1, 0)))
+    last = 4 * (jnp.maximum(z, line - 1 - z) - 2) + 2 + jnp.where(z < line - 1 - z, 1, 0)
+
+    def finish(d, k):
+        side = 2 * lax.rem(k, 2) - 1
+        zp = z + d * side
+        s = jnp.where(k < 2, other_y, y)
+
+        @pl.when((zp >= 0) & (zp < line) & ((d > 0) | (side > 0)))
+        def _():
+            rp = zp * 2 + s
+            p_copy(rp).wait_recv()
+            tile = (own_ref[rp] + part_ref[rp].astype(jnp.float32)).T
+            for block_index in range(n_row):
+                @pl.when(rp == block_index)
+                def _():
+                    out_ref[:, block_index * block:(block_index + 1) * block] = tile
+
+    def finish_all(d):
+        def step(k, carry):
+            finish(d, k)
+            return carry
+
+        lax.fori_loop(0, 4, step, 0)
 
     def single(t, carry):
         d = t // 4 + 2
@@ -232,9 +253,14 @@
             home = lax.dot_general(cols[zp, s], weighted[y], NT, preferred_element_type=jnp.float32)
             own_ref[rp] = home
             q[0] += lax.dot_general(v, home.astype(jnp.bfloat16), NN, preferred_element_type=jnp.float32)
+
+        @pl.when(lax.rem(t, 4) == 3)
+        def _():
+            finish_all(d - 2)
         return carry
 
     lax.fori_loop(0, slots, single, 0)
+    finish_all(line - 2)
     q_copy.wait()
     total = q[0] + qrecv[...].astype(jnp.float32)
     for cp in range(n_col):
@@ -259,6 +285,7 @@
     diagonal = jnp.where(lane_slot + 0.5 < limit, energies_ref[...], 0.0)
     prod_ref[...] = answer + diagonal * vt_ref[...].astype(jnp.float32)
 
+    finish_all(line - 1)
     y_copy().wait_send()
     for step in range(1, n_col):
         c_copy(step).wait_send()
@@ -278,13 +305,7 @@
             def _():
                 down(d_ref.at[0], zp, s).wait_send()
     for rp in range(n_row):
-        p_copy(rp).wait()
-
-
-def assemble_kernel(own_ref, part_ref, out_ref):
-    n_row, rows, chunk = own_ref.shape
-    total = own_ref[...] + part_ref[...].astype(jnp.float32)
-    out_ref[...] = total.reshape(n_row * rows, chunk).T
+        p_copy(rp).wait_send()
 
 
 def body(n_row, n_col, densities, counts, coulomb, energies, vectors):
@@ -297,16 +318,17 @@
     vmem = pl.BlockSpec(memory_space=pltpu.VMEM)
     dma = pltpu.SemaphoreType.DMA
     wide = n_col * rows
-    own, part, prod = pl.pallas_call(
+    kernel, prod = pl.pallas_call(
         functools.partial(exchange_kernel, n_row, n_col),
         out_shape=(
-            jax.ShapeDtypeStruct((n_row, rows, wide), f32),
-            jax.ShapeDtypeStruct((n_row, rows, wide), bf16),
+            jax.ShapeDtypeStruct((wide, n_row * rows), f32),
             jax.ShapeDtypeStruct((nv, rows), f32),
         ),
         in_specs=[vmem] * 5,
-        out_specs=(vmem, vmem, vmem),
+        out_specs=(vmem, vmem),
         scratch_shapes=[
+            pltpu.VMEM((n_row, rows, wide), f32),
+            pltpu.VMEM((n_row, rows, wide), bf16),
             pltpu.VMEM((2, rows, half), bf16),
             pltpu.VMEM(packed.shape, bf16),
             pltpu.VMEM((line, 2, rows, half), bf16),
@@ -327,14 +349,6 @@
         compiler_params=pltpu.CompilerParams(
             collective_id=0, has_side_effects=True, vmem_limit_bytes=60 * 2**20),
     )(densities, counts[None], energies[None], vectors.T, coulomb.reshape(2, 1, half))
-    chunk = 128
-    kernel = pl.pallas_call(
-        assemble_kernel,
-        out_shape=jax.ShapeDtypeStruct((wide, n_row * rows), f32),
-        grid=(pl.cdiv(wide, chunk),),
-        in_specs=[pl.BlockSpec((n_row, rows, chunk), lambda i: (0, 0, i))] * 2,
-        out_specs=pl.BlockSpec((chunk, n_row * rows), lambda i: (i, 0)),
-    )(own, part)
     return (kernel, prod.T)
 
 

time: 86.1 us -> 84.2 us (0.978)
  Pallas kernels: 84.6 us -> 79.3 us
  local copies, waits for them, and re-layouts: 0.63 us -> 4.09 us
    pallas_call x1 -> x0, Pallas kernels: 5.74 us -> none  [body(): pl.pallas_call(assemble_kernel, out_shape=jax.ShapeDtypeStruct((wide, n_r...]
    unnamed x3 -> x4, local copies, waits for them, and re-layouts: 0.63 us -> 4.09 us
where the time goes in v4:
time: 84.2 us; the launch traced here: 84.1 us
  Pallas kernels  79.3 us (94%)
  local copies, waits for them, and re-layouts  4.09 us (5%)
    pallas_call x1, Pallas kernels, body(): pl.pallas_call(functools.partial(exchange_kernel, n_row, n_col), out_shap...  79.3 us
    unnamed x4, local copies, waits for them, and re-layouts  4.09 us

profile of v4, /device:TPU:0, one launch (start us, length us, event | category | flops | bytes accessed | tf_op | source)
XLA Modules:
  0.0 84.1 jit_solution(13431905682069800035)
XLA Ops:
  0.6 79.3 %shard_map.68 = (f32[576,1152]{1,0:T(8,128)}, f32[64,144]{1,0:T(8,128)}) custom-call(bf16[144,3072]{1,0:T(8,128)(2,1)} %raw_ref.1, s32[1,16]{1,0:T(1,128)} %bitcast.9, f32[1,144]{1,0:T(1,128)} %bitcast.8, bf16[64,144]{1,0:T(8,128)(2,1)} %bitcast.6, f32[2,1,1536]{2,1,0:T(1,128)} %bitcast.7), custom_call_target="tpu_custom_call" | custom-call | tf_op jit(solution)/shard_map/pallas_call | solution.py:321
  80.0 0.0 copy-start
  80.0 3.5 %copy.9 = f32[576,1152]{1,0:T(8,128)} copy(f32[576,1152]{1,0:T(8,128)} %get-tuple-element.8) | data formatting | bytes 5308416
  83.4 0.0 copy-done
  83.4 0.6 copy.10
Async XLA Ops:
  80.0 3.5 %copy-start = (f32[64,144]{1,0:T(8,128)S(1)}, f32[64,144]{1,0:T(8,128)}, u32[]{:S(2)}) copy-start(f32[64,144]{1,0:T(8,128)} %get-tuple-element.5) | copy-start | bytes 110596

commit v5 on v4

--- a/solution.py
+++ b/solution.py
@@ -215,7 +215,7 @@
         def _():
             rp = zp * 2 + s
             p_copy(rp).wait_recv()
-            tile = (own_ref[rp] + part_ref[rp].astype(jnp.float32)).T
+            tile = (own_ref[rp] + part_ref[rp].astype(jnp.float32)).T.astype(jnp.bfloat16)
             for block_index in range(n_row):
                 @pl.when(rp == block_index)
                 def _():
@@ -254,13 +254,16 @@
             own_ref[rp] = home
             q[0] += lax.dot_general(v, home.astype(jnp.bfloat16), NN, preferred_element_type=jnp.float32)
 
-        @pl.when(lax.rem(t, 4) == 3)
+        @pl.when(lax.rem(t, 4) == 1)
         def _():
             finish_all(d - 2)
+
+        @pl.when(t == slots - 3)
+        def _():
+            finish_all(line - 2)
         return carry
 
     lax.fori_loop(0, slots, single, 0)
-    finish_all(line - 2)
     q_copy.wait()
     total = q[0] + qrecv[...].astype(jnp.float32)
     for cp in range(n_col):
@@ -321,7 +324,7 @@
     kernel, prod = pl.pallas_call(
         functools.partial(exchange_kernel, n_row, n_col),
         out_shape=(
-            jax.ShapeDtypeStruct((wide, n_row * rows), f32),
+            jax.ShapeDtypeStruct((wide, n_row * rows), bf16),
             jax.ShapeDtypeStruct((nv, rows), f32),
         ),
         in_specs=[vmem] * 5,
@@ -349,7 +352,7 @@
         compiler_params=pltpu.CompilerParams(
             collective_id=0, has_side_effects=True, vmem_limit_bytes=60 * 2**20),
     )(densities, counts[None], energies[None], vectors.T, coulomb.reshape(2, 1, half))
-    return (kernel, prod.T)
+    return (kernel.astype(f32), prod.T)
 
 
 def solution(mesh):

time: 84.2 us -> 83.1 us (0.987)
  local copies, waits for them, and re-layouts: 4.09 us -> 0.63 us
  other arithmetic: 0 us -> 3.04 us
    unnamed x4 -> x3, local copies, waits for them, and re-layouts: 4.09 us -> 0.63 us
    convert_element_type x0 -> x1, other arithmetic: none -> 3.04 us  [body(): return (kernel.astype(f32), prod.T)]
where the time goes in v5:
time: 83.1 us; the launch traced here: 83 us
  Pallas kernels  78.6 us (95%)
  other arithmetic  3.04 us (4%)
    pallas_call x1, Pallas kernels, body(): pl.pallas_call(functools.partial(exchange_kernel, n_row, n_col), out_shap...  78.6 us
    convert_element_type x1, other arithmetic, body(): return (kernel.astype(f32), prod.T)  3.04 us

profile of v5, /device:TPU:0, one launch (start us, length us, event | category | flops | bytes accessed | tf_op | source)
XLA Modules:
  0.0 83.0 jit_solution(3359359552664236300)
XLA Ops:
  0.6 78.6 %shard_map.68 = (bf16[576,1152]{1,0:T(8,128)(2,1)}, f32[64,144]{1,0:T(8,128)}) custom-call(bf16[144,3072]{1,0:T(8,128)(2,1)} %raw_ref.1, s32[1,16]{1,0:T(1,128)} %bitcast.9, f32[1,144]{1,0:T(1,128)} %bitcast.8, bf16[64,144]{1,0:T(8,128)(2,1)} %bitcast.6, f32[2,1,1536]{2,1,0:T(1,128)} %bitcast.7), custom_call_target="tpu_custom_call" | custom-call | tf_op jit(solution)/shard_map/pallas_call | solution.py:324
  79.3 0.0 copy-start
  79.3 3.0 %convert_element_type.3 = f32[576,1152]{1,0:T(8,128)} convert(bf16[576,1152]{1,0:T(8,128)(2,1)} %get-tuple-element.4) | non-fusion elementwise | flops 663552 | bytes 3981312 | tf_op jit(solution)/shard_map/convert_element_type | solution.py:355
  82.3 0.0 copy-done
  82.3 0.6 copy.8
Async XLA Ops:
  79.3 3.1 %copy-start = (f32[64,144]{1,0:T(8,128)S(1)}, f32[64,144]{1,0:T(8,128)}, u32[]{:S(2)}) copy-start(f32[64,144]{1,0:T(8,128)} %get-tuple-element.5) | copy-start | bytes 110596
